TPU v7x, 32 devices: a whole 2x2x4 slice. The times are simulated.
32 devices in a mesh: section: 2 (over core), seq: 4 (over y, x), mp: 4 (over z).
Axes of the slice: x: 2, y: 2, z: 4, core: 2. Of those that a mesh axis runs over, the one named last changes fastest.
Arguments:
- token_ids: int32 [2, 1024], P(None, 'seq'), may hold values from 0 to 511
- embed_table: bfloat16 [512, 4096], P(None, 'mp'), may hold values from -40 to 40
- norm_gain: bfloat16 [2, 4096], P('section', 'mp'), may hold values from 0.099609375 to 1.8984375
- short_filters: bfloat16 [2, 3, 7, 4096], P('section', None, None, 'mp'), may hold values from -2 to 2
- medium_filters: bfloat16 [2, 128, 4096], P('section', None, 'mp'), may hold values from -0.5 to 0.5
- out_weight: bfloat16 [2, 4096, 4096], P('section', 'seq', 'mp'), may hold values from -0.09375 to 0.09375
Outputs:
- streams: bfloat16 [2, 2, 1024, 4096], P('section', None, 'seq', 'mp')
All inputs are finite; a program needn't handle non-finite values.
Results may differ from a plain program's by a relative error of at most 0.018.
Values may be sent and summed in bfloat16 or wider, within the bound.
A program may use at most 64 MiB of HBM per device.

v0:
```python
import jax
import jax.numpy as jnp
from jax import lax
from jax.sharding import PartitionSpec as P

D = 4096


def passed_along(value, axis, by):
    devices = lax.axis_size(axis)
    pairs = [(i, i + by) for i in range(devices) if 0 <= i + by < devices]
    return lax.ppermute(value, axis, pairs)


def depthwise(extended, taps):
    kernel = jnp.flip(taps, 0)[:, None, :]
    result = lax.conv_general_dilated(
        extended[None],
        kernel,
        (1,),
        "VALID",
        dimension_numbers=("NWC", "WIO", "NWC"),
        feature_group_count=taps.shape[1],
        preferred_element_type=jnp.float32,
    )
    return result[0]


def mixer_layer(stream_in, gain, shorts, medium, weight_cols):
    rows = stream_in.shape[0]
    stream = stream_in.astype(jnp.float32)
    own_squares = jnp.sum(stream * stream, axis=1, keepdims=True)
    all_squares = lax.psum(own_squares, "mp")
    normed = (
        stream * lax.rsqrt(all_squares / D + 1e-06) * gain.astype(jnp.float32)[None, :]
    ).astype(jnp.bfloat16)
    short_span = shorts.shape[1] - 1
    medium_span = medium.shape[0] - 1
    lower_rim = passed_along(normed[rows - short_span :], "seq", 1)
    extended = jnp.concatenate([lower_rim, normed], axis=0)
    features = [depthwise(extended, shorts[index]).astype(jnp.bfloat16) for index in range(3)]
    product = (features[1].astype(jnp.float32) * features[2].astype(jnp.float32)).astype(
        jnp.bfloat16
    )
    product_rim = passed_along(product[rows - medium_span :], "seq", 1)
    filtered = depthwise(jnp.concatenate([product_rim, product], axis=0), medium)
    query = features[0]
    gated = (query.astype(jnp.float32) * filtered).astype(jnp.bfloat16)
    empty = jnp.zeros((rows, weight_cols.shape[1]), jnp.float32)
    piece = jax.tree.map(lambda a: lax.all_gather(a, "mp", axis=1, tiled=True), gated)
    block_rows = lax.slice_in_dim(weight_cols, 0, piece.shape[1], axis=0)
    projected = empty + jnp.dot(piece, block_rows, preferred_element_type=jnp.float32)
    return (stream + projected).astype(jnp.bfloat16)


def local(token_ids, embed_table, norm_gain, short_filters, medium_filters, out_weight):
    section_index = lax.axis_index("section")
    weight_cols = lax.all_gather(out_weight, "seq", axis=1, tiled=True)[0]
    gain = norm_gain[0]
    shorts = short_filters[0]
    medium = medium_filters[0]
    micro_count = token_ids.shape[0]
    rows = token_ids.shape[1]
    width = embed_table.shape[1]
    vocab_ids = lax.broadcasted_iota(jnp.int32, (rows, embed_table.shape[0]), 1)
    received = jnp.zeros((rows, width), jnp.bfloat16)
    results = []
    for tick_index in range(micro_count + 1):
        chosen = token_ids[min(tick_index, micro_count - 1)]
        one_hot = (chosen[:, None] == vocab_ids).astype(jnp.bfloat16)
        embedded = jnp.dot(one_hot, embed_table, preferred_element_type=jnp.float32).astype(
            jnp.bfloat16
        )
        stream_in = jnp.where(section_index == 0, embedded, received)
        result = mixer_layer(stream_in, gain, shorts, medium, weight_cols)
        results.append(result)
        if tick_index < micro_count:
            received = passed_along(result, "section", 1)
    ordered = [
        jnp.where(section_index == 0, results[index], results[index + 1])
        for index in range(micro_count)
    ]
    return jnp.stack(ordered)[None]


def solution(mesh):
    in_specs = (
        P(None, "seq"),
        P(None, "mp"),
        P("section", "mp"),
        P("section", None, None, "mp"),
        P("section", None, "mp"),
        P("section", "seq", "mp"),
    )
    out_specs = P("section", None, "seq", "mp")
    return jax.shard_map(local, mesh=mesh, in_specs=in_specs, out_specs=out_specs, check_vma=False)
```

profile of v0, /device:TPU:0, one launch (start us, length us, event | category | flops | bytes accessed | tf_op | source)
XLA Modules:
  0.0 514.0 jit_solution(5375181700684785683)
XLA Ops:
  8.6 13.5 %psum.21 = f32[256,1]{0,1:T(1,128)S(1)} all-reduce(f32[256,1]{0,1:T(1,128)S(1)} %bitcast.136), channel_id=1, replica_groups=mesh['section'=2,'seq'=4,'mp'=4] {'mp'}, use_global_device_ids=true, to_apply=%region_1.2 | all-reduce | flops 256 | bytes 2048 | tf_op jit(solution)/shard_map/psum | solution.py:33
  22.3 3.4 collective-permute-start
  26.5 2.6 rev.25
  32.5 4.1 collective-permute-start.1
  37.9 2.3 reshape.126
  41.5 15.2 %fusion.86 = bf16[1,256,1024]{2,0,1:T(2,128)(2,1)} fusion(bf16[1,383,1024]{2,1,0:T(8,128)(2,1)S(1)} %maximum_bitcast_fusion.1, f32[1,264,1024]{2,0,1:T(1,128)S(1)} %copy-done.2, bf16[128,1,1024]{2,0,1:T(8,128)(2,1)S(1)} %bitcast.116), kind=kOutput, calls=%fused_computation.73 | convolution fusion | flops 67633152 | bytes 2619392 | tf_op jit(solution)/shard_map/conv_general_dilated | solution.py:17
  58.0 78.3 %all-gather.10.cloned.1.call-done = bf16[1,256,4096]{2,0,1:T(2,128)(2,1)} async-done(((bf16[1,256,1024]{2,0,1:T(2,128)(2,1)}), bf16[1,256,4096]{2,0,1:T(2,128)(2,1)}) %all-gather.10.cloned.1.call-update) | async-done | bytes 2097168 | tf_op jit(solution)/shard_map/all_gather | solution.py:50
  136.3 87.5 %all-gather.8.cloned.1.call-done = bf16[1,4096,1024]{2,1,0:T(8,128)(2,1)} async-done(((bf16[1,1024,1024]{2,1,0:T(8,128)(2,1)}), bf16[1,4096,1024]{2,1,0:T(8,128)(2,1)}) %all-gather.8.cloned.1.call-update) | async-done | bytes 8388624 | tf_op jit(solution)/shard_map/all_gather | solution.py:58
  223.8 8.6 %fusion.54 = bf16[256,1024]{1,0:T(8,128)(2,1)S(1)} fusion(bf16[1,4096,1024]{2,1,0:T(8,128)(2,1)} %all-gather.8.cloned.1.call-done, bf16[1,256,4096]{2,0,1:T(2,128)(2,1)} %all-gather.10.cloned.1.call-done, bf16[256,1024]{1,0:T(8,128)(2,1)S(1)} %get-tuple-element.15), kind=kOutput, calls=%fused_computation.62 | convolution fusion | flops 2148270080 | bytes 11534336 | tf_op jit(solution)/shard_map/dot_general | solution.py:52
  232.5 1.6 collective-permute-start.2
  234.1 1.5 collective-permute-done.2
  236.2 11.7 %psum.22 = f32[256,1]{0,1:T(1,128)S(1)} all-reduce(f32[256,1]{0,1:T(1,128)S(1)} %bitcast.135), channel_id=1, replica_groups=mesh['section'=2,'seq'=4,'mp'=4] {'mp'}, use_global_device_ids=true, to_apply=%region_3.4 | all-reduce | flops 256 | bytes 2048 | tf_op jit(solution)/shard_map/psum | solution.py:33
  248.1 3.4 collective-permute-start.3
  256.2 4.9 collective-permute-start.4
  265.7 15.2 %fusion.92 = bf16[1,256,1024]{2,0,1:T(2,128)(2,1)} fusion(bf16[1,383,1024]{2,1,0:T(8,128)(2,1)S(1)} %maximum_bitcast_fusion.2, f32[1,264,1024]{2,0,1:T(1,128)S(1)} %reshape.127, bf16[128,1,1024]{2,0,1:T(8,128)(2,1)S(1)} %bitcast.117), kind=kOutput, calls=%fused_computation.75 | convolution fusion | flops 67633152 | bytes 2619392 | tf_op jit(solution)/shard_map/conv_general_dilated | solution.py:17
  281.1 80.5 %all-gather.12.cloned.1.call-done = bf16[1,256,4096]{2,0,1:T(2,128)(2,1)} async-done(((bf16[1,256,1024]{2,0,1:T(2,128)(2,1)}), bf16[1,256,4096]{2,0,1:T(2,128)(2,1)}) %all-gather.12.cloned.1.call-update) | async-done | bytes 2097168 | tf_op jit(solution)/shard_map/all_gather | solution.py:50
  361.6 8.6 %fusion.59 = bf16[256,1024]{1,0:T(8,128)(2,1)S(1)} fusion(bf16[1,4096,1024]{2,1,0:T(8,128)(2,1)} %all-gather.8.cloned.1.call-done, bf16[1,256,4096]{2,0,1:T(2,128)(2,1)} %all-gather.12.cloned.1.call-done, bf16[256,1024]{1,0:T(8,128)(2,1)S(1)} %copy-done.4), kind=kOutput, calls=%fused_computation.63 | convolution fusion | flops 2148270080 | bytes 11534336 | tf_op jit(solution)/shard_map/dot_general | solution.py:52
  371.6 1.5 collective-permute-done.5
  373.3 9.4 %psum.23 = f32[256,1]{0,1:T(1,128)S(1)} all-reduce(f32[256,1]{0,1:T(1,128)S(1)} %bitcast.131), channel_id=1, replica_groups=mesh['section'=2,'seq'=4,'mp'=4] {'mp'}, use_global_device_ids=true, to_apply=%region_5.6 | all-reduce | flops 256 | bytes 2048 | tf_op jit(solution)/shard_map/psum | solution.py:33
  382.9 3.4 collective-permute-start.6
  391.0 5.1 collective-permute-start.7
  400.5 15.2 %fusion.98 = bf16[1,256,1024]{2,0,1:T(2,128)(2,1)} fusion(bf16[1,383,1024]{2,1,0:T(8,128)(2,1)S(1)} %maximum_bitcast_fusion.3, f32[1,264,1024]{2,0,1:T(1,128)S(1)} %reshape.128, bf16[128,1,1024]{2,0,1:T(8,128)(2,1)S(1)} %bitcast.118), kind=kOutput, calls=%fused_computation.77 | convolution fusion | flops 67633152 | bytes 2619392 | tf_op jit(solution)/shard_map/conv_general_dilated | solution.py:17
  416.9 80.5 %all-gather.14.cloned.1.call-done = bf16[1,256,4096]{2,0,1:T(2,128)(2,1)} async-done(((bf16[1,256,1024]{2,0,1:T(2,128)(2,1)}), bf16[1,256,4096]{2,0,1:T(2,128)(2,1)}) %all-gather.14.cloned.1.call-update) | async-done | bytes 2097168 | tf_op jit(solution)/shard_map/all_gather | solution.py:50
  497.4 8.7 %fusion.78 = bf16[1,256,1024]{2,1,0:T(8,128)(2,1)S(1)} fusion(bf16[256,1024]{1,0:T(8,128)(2,1)S(1)} %copy-done.8, bf16[1,4096,1024]{2,1,0:T(8,128)(2,1)} %all-gather.8.cloned.1.call-done, bf16[1,256,4096]{2,0,1:T(2,128)(2,1)} %all-gather.14.cloned.1.call-done, bf16[256,1024]{1,0:T(8,128)(2,1)S(1)} %get-tuple-element.6, pred[]{:T(512)S(6)} %eq.14), kind=kOutput, calls=%fused_computation.71 | convolution fusion | flops 2148532224 | bytes 12058625 | tf_op jit(solution)/shard_map/dot_general | solution.py:52
  (109 shorter events, 33.5 us)
Async XLA Ops:
  6.5 1.5 copy-start
  6.5 129.7 %all-gather.10.cloned.1.call-start = ((), (), s32[]{:S(2)}) async-start(), calls=%async_computation.1 | async-start | bytes 5242880 | tf_op jit(solution)/shard_map/all_gather | solution.py:50
  8.0 17.7 %copy-start.13 = (bf16[1,3,7,1024]{3,2,1,0:T(8,128)(2,1)S(1)}, bf16[1,3,7,1024]{3,2,1,0:T(8,128)(2,1)}, u32[]{:S(2)}) copy-start(bf16[1,3,7,1024]{3,2,1,0:T(8,128)(2,1)} %param.9) | copy-start | bytes 129028
  8.0 18.5 %copy-start.9 = (bf16[1,128,1024]{2,1,0:T(8,128)(2,1)S(1)}, bf16[1,128,1024]{2,1,0:T(8,128)(2,1)}, u32[]{:S(2)}) copy-start(bf16[1,128,1024]{2,1,0:T(8,128)(2,1)} %param.10) | copy-start | bytes 786436
  22.3 6.8 %collective-permute-start = (bf16[6,1024]{1,0:T(8,128)(2,1)S(1)}, bf16[6,1024]{1,0:T(8,128)(2,1)S(1)}, u32[]{:S(2)}, u32[]{:S(2)}) collective-permute-start(bf16[6,1024]{1,0:T(8,128)(2,1)S(1)} %slice.84), channel_id=1, source_target_pairs={{0,4},{4,8},{8,12},{1,5},{5,9},{9,13},{2,6},{6,10},{10,14},{3,7},{... | collective-permute-start | bytes 36872 | tf_op jit(solution)/shard_map/ppermute | solution.py:12
  32.5 7.7 %collective-permute-start.1 = (bf16[127,1024]{1,0:T(8,128)(2,1)}, bf16[127,1024]{1,0:T(8,128)(2,1)}, u32[]{:S(2)}, u32[]{:S(2)}) collective-permute-start(bf16[127,1024]{1,0:T(8,128)(2,1)} %slice_bitcast_fusion.5), channel_id=1, source_target_pairs={{0,4},{4,8},{8,12},{1,5},{5,9},{9,13},{2,6},{6,10},{10,14},{3,7},{... | collective-permute-start | bytes 780296 | tf_op jit(solution)/shard_map/ppermute | solution.py:12
  40.2 1.3 copy-start.2
  40.2 1.4 copy-start.10
  56.7 167.1 %all-gather.8.cloned.1.call-start = ((), (), s32[]{:S(2)}) async-start(), calls=%async_computation | async-start | bytes 10485760 | tf_op jit(solution)/shard_map/all_gather | solution.py:58
  57.5 304.1 %all-gather.12.cloned.1.call-start = ((), (), s32[]{:S(2)}) async-start(), calls=%async_computation.2 | async-start | bytes 5242880 | tf_op jit(solution)/shard_map/all_gather | solution.py:50
  232.5 3.1 copy-start.5
  232.5 3.1 collective-permute-start.2
  236.2 16.7 %copy-start.3 = (bf16[256,1024]{1,0:T(8,128)(2,1)}, bf16[256,1024]{1,0:T(8,128)(2,1)S(1)}, u32[]{:S(2)}) copy-start(bf16[256,1024]{1,0:T(8,128)(2,1)S(1)} %get-tuple-element.8) | copy-start | bytes 1572868
  248.1 4.8 collective-permute-start.3
  256.2 8.4 %collective-permute-start.4 = (bf16[127,1024]{1,0:T(8,128)(2,1)}, bf16[127,1024]{1,0:T(8,128)(2,1)}, u32[]{:S(2)}, u32[]{:S(2)}) collective-permute-start(bf16[127,1024]{1,0:T(8,128)(2,1)} %slice_bitcast_fusion.4), channel_id=1, source_target_pairs={{0,4},{4,8},{8,12},{1,5},{5,9},{9,13},{2,6},{6,10},{10,14},{3,7},{... | collective-permute-start | bytes 780296 | tf_op jit(solution)/shard_map/ppermute | solution.py:12
  263.6 2.0 copy-start.11
  265.6 95.9 %copy-start.4 = (bf16[256,1024]{1,0:T(8,128)(2,1)S(1)}, bf16[256,1024]{1,0:T(8,128)(2,1)}, u32[]{:S(2)}) copy-start(bf16[256,1024]{1,0:T(8,128)(2,1)} %copy-done.3) | copy-start | bytes 1572868
  280.9 216.5 %all-gather.14.cloned.1.call-start = ((), (), s32[]{:S(2)}) async-start(), calls=%async_computation.3 | async-start | bytes 5242880 | tf_op jit(solution)/shard_map/all_gather | solution.py:50
  370.2 12.7 %copy-start.7 = (bf16[256,1024]{1,0:T(8,128)(2,1)}, bf16[256,1024]{1,0:T(8,128)(2,1)S(1)}, u32[]{:S(2)}) copy-start(bf16[256,1024]{1,0:T(8,128)(2,1)S(1)} %fusion.59) | copy-start | bytes 1572868
  370.2 2.8 collective-permute-start.5
  382.9 4.8 collective-permute-start.6
  391.0 8.4 %collective-permute-start.7 = (bf16[127,1024]{1,0:T(8,128)(2,1)}, bf16[127,1024]{1,0:T(8,128)(2,1)}, u32[]{:S(2)}, u32[]{:S(2)}) collective-permute-start(bf16[127,1024]{1,0:T(8,128)(2,1)} %slice_bitcast_fusion.3), channel_id=1, source_target_pairs={{0,4},{4,8},{8,12},{1,5},{5,9},{9,13},{2,6},{6,10},{10,14},{3,7},{... | collective-permute-start | bytes 780296 | tf_op jit(solution)/shard_map/ppermute | solution.py:12
  398.7 1.8 copy-start.12
  497.4 9.8 %copy-start.1 = (bf16[512,1024]{1,0:T(8,128)(2,1)S(1)}, bf16[512,1024]{1,0:T(8,128)(2,1)}, u32[]{:S(2)}) copy-start(bf16[512,1024]{1,0:T(8,128)(2,1)} %param.7) | copy-start | bytes 3145732
  (3 other events, 2.9 us)
Sparse Core Ops, SparseCore 0:
  56.8 79.4 all-gather.9
  138.1 85.6 all-gather.7
  281.0 80.5 all-gather.11
  415.8 81.5 all-gather.13
where the time goes:
time: 521 us; the launch traced here: 514 us
  waiting for transfers between devices  335 us (64%)
  matrix products  78.3 us (15%)
  blocking collectives  34.5 us (7%)
  starting transfers between devices  27.9 us (5%)
  local copies, waits for them, and re-layouts  18 us (3%)
  between operations  13.9 us (3%)
  other arithmetic  6.4 us (1%)
    all_gather x3, waiting for transfers between devices, mixer_layer(): lax.all_gather(a, 'mp', axis=1, tiled=True)  239 us
    all_gather x1, waiting for transfers between devices, local(): weight_cols = lax.all_gather(out_weight, 'seq', axis=1, tiled=True)[0]  87.5 us
    conv_general_dilated x12, matrix products, depthwise(): lax.conv_general_dilated(extended[None], kernel, (1,), 'VALID', dimension...  51.1 us
    psum x3, blocking collectives, mixer_layer(): all_squares = lax.psum(own_squares, 'mp')  34.5 us
    ppermute x8, starting transfers between devices, passed_along(): return lax.ppermute(value, axis, pairs)  27.2 us
    dot_general x3, matrix products, mixer_layer(): jnp.dot(piece, block_rows, preferred_element_type=jnp.float32)  26 us
  transfers between devices with their start and end apart: 12, of which 10 were waited for; matrix products, arithmetic and copies ran while one was open for 2% of the time, Pallas kernels for 0%

commit v1 on v0

--- a/solution.py
+++ b/solution.py
@@ -30,7 +30,11 @@
     rows = stream_in.shape[0]
     stream = stream_in.astype(jnp.float32)
     own_squares = jnp.sum(stream * stream, axis=1, keepdims=True)
-    all_squares = lax.psum(own_squares, "mp")
+    all_squares = own_squares
+    for hop in (1, 2):
+        all_squares = all_squares + lax.ppermute(
+            all_squares, "mp", [(dev, dev ^ hop) for dev in range(4)]
+        )
     normed = (
         stream * lax.rsqrt(all_squares / D + 1e-06) * gain.astype(jnp.float32)[None, :]
     ).astype(jnp.bfloat16)

time: 521 us -> 517 us (level)
  blocking collectives: 34.5 us -> 0 us
  waiting for transfers between devices: 335 us -> 353 us
  starting transfers between devices: 27.9 us -> 41.1 us
    psum x3 -> x0, blocking collectives: 34.5 us -> none  [mixer_layer(): all_squares = lax.psum(own_squares, 'mp')]
    ppermute x0 -> x6, waiting for transfers between devices: none -> 13.1 us  [mixer_layer(): lax.ppermute(all_squares, 'mp', [(dev, dev ^ hop) for dev in range(4)])]
    ppermute x0 -> x6, starting transfers between devices: none -> 12.3 us  [mixer_layer(): lax.ppermute(all_squares, 'mp', [(dev, dev ^ hop) for dev in range(4)])]
  transfers between devices with their start and end apart: 12 -> 18, of which waited for: 10 -> 16; matrix products, arithmetic and copies ran while one was open for 2% -> 2% of each run, Pallas kernels for 0% -> 0%
where the time goes in v1:
time: 517 us; the launch traced here: 510 us
  waiting for transfers between devices  353 us (68%)
  matrix products  78.3 us (15%)
  starting transfers between devices  41.1 us (8%)
  local copies, waits for them, and re-layouts  18.4 us (4%)
  between operations  13.9 us (3%)
  other arithmetic  5.71 us (1%)
    all_gather x3, waiting for transfers between devices, mixer_layer(): lax.all_gather(a, 'mp', axis=1, tiled=True)  244 us
    all_gather x1, waiting for transfers between devices, local(): weight_cols = lax.all_gather(out_weight, 'seq', axis=1, tiled=True)[0]  87.5 us
    conv_general_dilated x12, matrix products, depthwise(): lax.conv_general_dilated(extended[None], kernel, (1,), 'VALID', dimension...  51.1 us
    ppermute x8, starting transfers between devices, passed_along(): return lax.ppermute(value, axis, pairs)  28 us
    dot_general x3, matrix products, mixer_layer(): jnp.dot(piece, block_rows, preferred_element_type=jnp.float32)  26 us
    ppermute x6, waiting for transfers between devices, mixer_layer(): lax.ppermute(all_squares, 'mp', [(dev, dev ^ hop) for dev in range(4)])  13.1 us
    ppermute x6, starting transfers between devices, mixer_layer(): lax.ppermute(all_squares, 'mp', [(dev, dev ^ hop) for dev in range(4)])  12.3 us
  transfers between devices with their start and end apart: 18, of which 16 were waited for; matrix products, arithmetic and copies ran while one was open for 2% of the time, Pallas kernels for 0%

profile of v1, /device:TPU:0, one launch (start us, length us, event | category | flops | bytes accessed | tf_op | source)
XLA Modules:
  0.0 510.4 jit_solution(7344661634316912493)
XLA Ops:
  8.4 3.1 collective-permute-start
  13.0 3.0 collective-permute-start.1
  17.8 3.7 collective-permute-start.2
  22.4 2.6 rev.25
  28.4 4.1 collective-permute-start.3
  33.7 2.3 reshape.126
  37.4 15.2 %fusion.86 = bf16[1,256,1024]{2,0,1:T(2,128)(2,1)} fusion(bf16[1,383,1024]{2,1,0:T(8,128)(2,1)S(1)} %maximum_bitcast_fusion.1, f32[1,264,1024]{2,0,1:T(1,128)S(1)} %copy-done.2, bf16[128,1,1024]{2,0,1:T(8,128)(2,1)S(1)} %bitcast.116), kind=kOutput, calls=%fused_computation.73 | convolution fusion | flops 67633152 | bytes 2619392 | tf_op jit(solution)/shard_map/conv_general_dilated | solution.py:17
  53.8 81.4 %all-gather.10.cloned.1.call-done = bf16[1,256,4096]{2,0,1:T(2,128)(2,1)} async-done(((bf16[1,256,1024]{2,0,1:T(2,128)(2,1)}), bf16[1,256,4096]{2,0,1:T(2,128)(2,1)}) %all-gather.10.cloned.1.call-update) | async-done | bytes 2097168 | tf_op jit(solution)/shard_map/all_gather | solution.py:54
  135.2 87.5 %all-gather.8.cloned.1.call-done = bf16[1,4096,1024]{2,1,0:T(8,128)(2,1)} async-done(((bf16[1,1024,1024]{2,1,0:T(8,128)(2,1)}), bf16[1,4096,1024]{2,1,0:T(8,128)(2,1)}) %all-gather.8.cloned.1.call-update) | async-done | bytes 8388624 | tf_op jit(solution)/shard_map/all_gather | solution.py:62
  222.8 8.6 %fusion.54 = bf16[256,1024]{1,0:T(8,128)(2,1)S(1)} fusion(bf16[1,4096,1024]{2,1,0:T(8,128)(2,1)} %all-gather.8.cloned.1.call-done, bf16[1,256,4096]{2,0,1:T(2,128)(2,1)} %all-gather.10.cloned.1.call-done, bf16[256,1024]{1,0:T(8,128)(2,1)S(1)} %get-tuple-element.15), kind=kOutput, calls=%fused_computation.62 | convolution fusion | flops 2148270080 | bytes 11534336 | tf_op jit(solution)/shard_map/dot_general | solution.py:56
  238.7 2.4 collective-permute-start.6
  243.4 3.4 collective-permute-start.7
  251.5 4.9 collective-permute-start.8
  261.0 15.2 %fusion.92 = bf16[1,256,1024]{2,0,1:T(2,128)(2,1)} fusion(bf16[1,383,1024]{2,1,0:T(8,128)(2,1)S(1)} %maximum_bitcast_fusion.2, f32[1,264,1024]{2,0,1:T(1,128)S(1)} %reshape.127, bf16[128,1,1024]{2,0,1:T(8,128)(2,1)S(1)} %bitcast.117), kind=kOutput, calls=%fused_computation.75 | convolution fusion | flops 67633152 | bytes 2619392 | tf_op jit(solution)/shard_map/conv_general_dilated | solution.py:17
  276.4 83.3 %all-gather.12.cloned.1.call-done = bf16[1,256,4096]{2,0,1:T(2,128)(2,1)} async-done(((bf16[1,256,1024]{2,0,1:T(2,128)(2,1)}), bf16[1,256,4096]{2,0,1:T(2,128)(2,1)}) %all-gather.12.cloned.1.call-update) | async-done | bytes 2097168 | tf_op jit(solution)/shard_map/all_gather | solution.py:54
  359.7 8.6 %fusion.59 = bf16[256,1024]{1,0:T(8,128)(2,1)S(1)} fusion(bf16[1,4096,1024]{2,1,0:T(8,128)(2,1)} %all-gather.8.cloned.1.call-done, bf16[1,256,4096]{2,0,1:T(2,128)(2,1)} %all-gather.12.cloned.1.call-done, bf16[256,1024]{1,0:T(8,128)(2,1)S(1)} %copy-done.4), kind=kOutput, calls=%fused_computation.63 | convolution fusion | flops 2148270080 | bytes 11534336 | tf_op jit(solution)/shard_map/dot_general | solution.py:56
  371.5 3.6 collective-permute-done.10
  375.1 2.1 collective-permute-start.11
  377.2 2.3 collective-permute-done.11
  379.8 3.9 collective-permute-start.12
  388.4 5.1 %collective-permute-start.13 = (bf16[127,1024]{1,0:T(8,128)(2,1)}, bf16[127,1024]{1,0:T(8,128)(2,1)}, u32[]{:S(2)}, u32[]{:S(2)}) collective-permute-start(bf16[127,1024]{1,0:T(8,128)(2,1)} %slice_bitcast_fusion.3), channel_id=1, source_target_pairs={{0,4},{4,8},{8,12},{1,5},{5,9},{9,13},{2,6},{6,10},{10,14},{3,7},{... | collective-permute-start | bytes 780296 | tf_op jit(solution)/shard_map/ppermute | solution.py:12
  397.9 15.2 %fusion.98 = bf16[1,256,1024]{2,0,1:T(2,128)(2,1)} fusion(bf16[1,383,1024]{2,1,0:T(8,128)(2,1)S(1)} %maximum_bitcast_fusion.3, f32[1,264,1024]{2,0,1:T(1,128)S(1)} %reshape.128, bf16[128,1,1024]{2,0,1:T(8,128)(2,1)S(1)} %bitcast.118), kind=kOutput, calls=%fused_computation.77 | convolution fusion | flops 67633152 | bytes 2619392 | tf_op jit(solution)/shard_map/conv_general_dilated | solution.py:17
  414.3 79.5 %all-gather.14.cloned.1.call-done = bf16[1,256,4096]{2,0,1:T(2,128)(2,1)} async-done(((bf16[1,256,1024]{2,0,1:T(2,128)(2,1)}), bf16[1,256,4096]{2,0,1:T(2,128)(2,1)}) %all-gather.14.cloned.1.call-update) | async-done | bytes 2097168 | tf_op jit(solution)/shard_map/all_gather | solution.py:54
  493.8 8.7 %fusion.78 = bf16[1,256,1024]{2,1,0:T(8,128)(2,1)S(1)} fusion(bf16[256,1024]{1,0:T(8,128)(2,1)S(1)} %copy-done.8, bf16[1,4096,1024]{2,1,0:T(8,128)(2,1)} %all-gather.8.cloned.1.call-done, bf16[1,256,4096]{2,0,1:T(2,128)(2,1)} %all-gather.14.cloned.1.call-done, bf16[256,1024]{1,0:T(8,128)(2,1)S(1)} %get-tuple-element.6, pred[]{:T(512)S(6)} %eq.14), kind=kOutput, calls=%fused_computation.71 | convolution fusion | flops 2148532224 | bytes 12058625 | tf_op jit(solution)/shard_map/dot_general | solution.py:56
  (123 shorter events, 46.7 us)
Async XLA Ops:
  6.5 128.7 %all-gather.10.cloned.1.call-start = ((), (), s32[]{:S(2)}) async-start(), calls=%async_computation.1 | async-start | bytes 5242880 | tf_op jit(solution)/shard_map/all_gather | solution.py:54
  7.8 13.8 %copy-start.13 = (bf16[1,3,7,1024]{3,2,1,0:T(8,128)(2,1)S(1)}, bf16[1,3,7,1024]{3,2,1,0:T(8,128)(2,1)}, u32[]{:S(2)}) copy-start(bf16[1,3,7,1024]{3,2,1,0:T(8,128)(2,1)} %param.9) | copy-start | bytes 129028
  8.4 14.0 %copy-start.9 = (bf16[1,128,1024]{2,1,0:T(8,128)(2,1)S(1)}, bf16[1,128,1024]{2,1,0:T(8,128)(2,1)}, u32[]{:S(2)}) copy-start(bf16[1,128,1024]{2,1,0:T(8,128)(2,1)} %param.10) | copy-start | bytes 786436
  8.4 4.7 collective-permute-start
  13.0 4.6 collective-permute-start.1
  17.8 7.1 %collective-permute-start.2 = (bf16[6,1024]{1,0:T(8,128)(2,1)S(1)}, bf16[6,1024]{1,0:T(8,128)(2,1)S(1)}, u32[]{:S(2)}, u32[]{:S(2)}) collective-permute-start(bf16[6,1024]{1,0:T(8,128)(2,1)S(1)} %slice.84), channel_id=1, source_target_pairs={{0,4},{4,8},{8,12},{1,5},{5,9},{9,13},{2,6},{6,10},{10,14},{3,7},{... | collective-permute-start | bytes 36872 | tf_op jit(solution)/shard_map/ppermute | solution.py:12
  28.4 7.7 %collective-permute-start.3 = (bf16[127,1024]{1,0:T(8,128)(2,1)}, bf16[127,1024]{1,0:T(8,128)(2,1)}, u32[]{:S(2)}, u32[]{:S(2)}) collective-permute-start(bf16[127,1024]{1,0:T(8,128)(2,1)} %slice_bitcast_fusion.5), channel_id=1, source_target_pairs={{0,4},{4,8},{8,12},{1,5},{5,9},{9,13},{2,6},{6,10},{10,14},{3,7},{... | collective-permute-start | bytes 780296 | tf_op jit(solution)/shard_map/ppermute | solution.py:12
  52.6 170.2 %all-gather.8.cloned.1.call-start = ((), (), s32[]{:S(2)}) async-start(), calls=%async_computation | async-start | bytes 10485760 | tf_op jit(solution)/shard_map/all_gather | solution.py:62
  53.3 306.4 %all-gather.12.cloned.1.call-start = ((), (), s32[]{:S(2)}) async-start(), calls=%async_computation.2 | async-start | bytes 5242880 | tf_op jit(solution)/shard_map/all_gather | solution.py:54
  231.4 3.1 collective-permute-start.4
  235.1 13.1 %copy-start.3 = (bf16[256,1024]{1,0:T(8,128)(2,1)}, bf16[256,1024]{1,0:T(8,128)(2,1)S(1)}, u32[]{:S(2)}) copy-start(bf16[256,1024]{1,0:T(8,128)(2,1)S(1)} %get-tuple-element.8) | copy-start | bytes 1572868
  235.1 3.6 collective-permute-start.5
  238.7 4.5 collective-permute-start.6
  243.4 4.8 collective-permute-start.7
  251.5 8.4 %collective-permute-start.8 = (bf16[127,1024]{1,0:T(8,128)(2,1)}, bf16[127,1024]{1,0:T(8,128)(2,1)}, u32[]{:S(2)}, u32[]{:S(2)}) collective-permute-start(bf16[127,1024]{1,0:T(8,128)(2,1)} %slice_bitcast_fusion.4), channel_id=1, source_target_pairs={{0,4},{4,8},{8,12},{1,5},{5,9},{9,13},{2,6},{6,10},{10,14},{3,7},{... | collective-permute-start | bytes 780296 | tf_op jit(solution)/shard_map/ppermute | solution.py:12
  261.0 98.7 %copy-start.4 = (bf16[256,1024]{1,0:T(8,128)(2,1)S(1)}, bf16[256,1024]{1,0:T(8,128)(2,1)}, u32[]{:S(2)}) copy-start(bf16[256,1024]{1,0:T(8,128)(2,1)} %copy-done.3) | copy-start | bytes 1572868
  276.2 217.6 %all-gather.14.cloned.1.call-start = ((), (), s32[]{:S(2)}) async-start(), calls=%async_computation.3 | async-start | bytes 5242880 | tf_op jit(solution)/shard_map/all_gather | solution.py:54
  368.3 11.4 %copy-start.7 = (bf16[256,1024]{1,0:T(8,128)(2,1)}, bf16[256,1024]{1,0:T(8,128)(2,1)S(1)}, u32[]{:S(2)}) copy-start(bf16[256,1024]{1,0:T(8,128)(2,1)S(1)} %fusion.59) | copy-start | bytes 1572868
  368.4 2.8 collective-permute-start.9
  371.4 3.6 collective-permute-start.10
  375.1 4.5 collective-permute-start.11
  379.8 5.3 %collective-permute-start.12 = (bf16[6,1024]{1,0:T(8,128)(2,1)S(1)}, bf16[6,1024]{1,0:T(8,128)(2,1)S(1)}, u32[]{:S(2)}, u32[]{:S(2)}) collective-permute-start(bf16[6,1024]{1,0:T(8,128)(2,1)S(1)} %slice.94), channel_id=1, source_target_pairs={{0,4},{4,8},{8,12},{1,5},{5,9},{9,13},{2,6},{6,10},{10,14},{3,7},{... | collective-permute-start | bytes 36872 | tf_op jit(solution)/shard_map/ppermute | solution.py:12
  388.4 8.4 %collective-permute-start.13 = (bf16[127,1024]{1,0:T(8,128)(2,1)}, bf16[127,1024]{1,0:T(8,128)(2,1)}, u32[]{:S(2)}, u32[]{:S(2)}) collective-permute-start(bf16[127,1024]{1,0:T(8,128)(2,1)} %slice_bitcast_fusion.3), channel_id=1, source_target_pairs={{0,4},{4,8},{8,12},{1,5},{5,9},{9,13},{2,6},{6,10},{10,14},{3,7},{... | collective-permute-start | bytes 780296 | tf_op jit(solution)/shard_map/ppermute | solution.py:12
  493.8 9.8 %copy-start.1 = (bf16[512,1024]{1,0:T(8,128)(2,1)S(1)}, bf16[512,1024]{1,0:T(8,128)(2,1)}, u32[]{:S(2)}) copy-start(bf16[512,1024]{1,0:T(8,128)(2,1)} %param.7) | copy-start | bytes 3145732
  (10 other events, 23.3 us)
Sparse Core Ops, SparseCore 0:
  52.7 82.4 all-gather.9
  137.0 85.6 all-gather.7
  276.3 83.3 all-gather.11
  413.2 80.5 all-gather.13
